TPU v7x, 32 devices: a whole 2x2x4 slice. The times are simulated.
32 devices in a mesh: gx: 2 (over y), gy: 4 (over z), gz: 4 (over x, core).
Axes of the slice: x: 2, y: 2, z: 4, core: 2. Of those that a mesh axis runs over, the one named last changes fastest.
Arguments:
- density: float32 [24, 64, 512], P('gx', 'gy', 'gz'), may hold values from 0.5 to 8
- potential: float32 [24, 64, 512], P('gx', 'gy', 'gz'), may hold values from -6 to 6
Outputs:
- corrected: float32 [24, 64, 512], P('gx', 'gy', 'gz')
All inputs are finite; a program needn't handle non-finite values.
Results may differ from a plain program's by a relative error of at most 0.00005.
Values sent between devices are 32-bit elements; how exact they have to be, the bound alone decides.
A program may use at most 64 MiB of HBM per device.

v0:
```python
import jax
import jax.numpy as jnp
from jax import lax
from jax.sharding import PartitionSpec as P

SWEEPS = 2


def with_halo(cells, sides, width):
    for axis, dim in sides:
        count = lax.axis_size(axis)
        head = lax.slice_in_dim(cells, 0, width, axis=dim)
        tail = lax.slice_in_dim(cells, cells.shape[dim] - width, cells.shape[dim], axis=dim)
        cells = jnp.concatenate(
            [
                lax.ppermute(tail, axis, [(i, (i + 1) % count) for i in range(count)]),
                cells,
                lax.ppermute(head, axis, [((i + 1) % count, i) for i in range(count)]),
            ],
            axis=dim,
        )
    return cells


def inner_sum(padded):
    total = padded[2:, 1:-1, 1:-1] + padded[:-2, 1:-1, 1:-1]
    total = total + padded[1:-1, 2:, 1:-1] + padded[1:-1, :-2, 1:-1]
    return total + padded[1:-1, 1:-1, 2:] + padded[1:-1, 1:-1, :-2]


def colour(shape, offset):
    summed = lax.broadcasted_iota(jnp.int32, shape, 0) + lax.broadcasted_iota(jnp.int32, shape, 1)
    summed = summed + lax.broadcasted_iota(jnp.int32, shape, 2) + offset
    return summed % 2 == 0


def basis(count):
    rows = lax.broadcasted_iota(jnp.int32, (count, count), 0).astype(jnp.float32)
    cols = lax.broadcasted_iota(jnp.int32, (count, count), 1)
    freq = ((cols + 1) // 2).astype(jnp.float32)
    angle = 2.0 * jnp.pi * freq * rows / count
    full = jnp.sqrt(2.0 / count)
    single = 1.0 / jnp.sqrt(jnp.float32(count))
    top = 2 * ((cols + 1) // 2) == count
    table = jnp.where(cols % 2 == 1, jnp.cos(angle) * full, jnp.sin(angle) * full)
    table = jnp.where(top, jnp.cos(angle) * single, table)
    table = jnp.where(cols == 0, single, table)
    modes = ((jnp.arange(count, dtype=jnp.int32) + 1) // 2).astype(jnp.float32)
    return (table, 2.0 - 2.0 * jnp.cos(2.0 * jnp.pi * modes / count))


def coarse_solve(blocks, weight_x, weight_y, weight_z):
    nx, ny, nz = blocks.shape
    qx, lx = basis(nx)
    qy, ly = basis(ny)
    qz, lz = basis(nz)
    hi = lax.Precision.HIGHEST
    spectrum = jnp.einsum("ia,jb,kc,ijk->abc", qx, qy, qz, blocks, precision=hi)
    denom = (
        weight_x * lx[:, None, None] + weight_y * ly[None, :, None] + weight_z * lz[None, None, :]
    )
    zero = colour((nx, ny, nz), 0) & (
        lax.broadcasted_iota(jnp.int32, (nx, ny, nz), 0)
        + lax.broadcasted_iota(jnp.int32, (nx, ny, nz), 1)
        + lax.broadcasted_iota(jnp.int32, (nx, ny, nz), 2)
        == 0
    )
    safe = jnp.where(zero, jnp.float32(1.0), denom)
    spectrum = jnp.where(zero, jnp.float32(0.0), -spectrum / safe)
    return jnp.einsum("ia,jb,kc,abc->ijk", qx, qy, qz, spectrum, precision=hi)


def trim(field, depth):
    if depth == 0:
        return field
    return field[depth:-depth, depth:-depth, depth:-depth]


def source_pad(source):
    return with_halo(source, (("gx", 0), ("gy", 1), ("gz", 2)), 2 * SWEEPS)


def sectioned(field, padded_source):
    reach = 2 * SWEEPS
    current = with_halo(field, (("gx", 0), ("gy", 1), ("gz", 2)), reach + 1)
    depth = reach + 1
    for sweep in range(SWEEPS):
        shell = trim(current, 1)
        red_shell = colour(shell.shape, depth - 1)
        shell = jnp.where(
            red_shell, (inner_sum(current) - trim(padded_source, reach - depth + 1)) / 6.0, shell
        )
        inside = trim(shell, 1)
        red_inside = colour(inside.shape, depth - 2)
        current = jnp.where(
            red_inside, inside, (inner_sum(shell) - trim(padded_source, reach - depth + 2)) / 6.0
        )
        depth = depth - 2
    inside = trim(current, 1)
    leftover = trim(padded_source, reach) - (inner_sum(current) - 6.0 * inside)
    return (inside, leftover)


def smooth_section(field, padded_source):
    return sectioned(field, padded_source)


def body(density, potential):
    sizes = lax.axis_size("gx") * lax.axis_size("gy") * lax.axis_size("gz")
    total = lax.psum(jnp.sum(density), ("gx", "gy", "gz"))
    source = density - total / (density.size * sizes)
    padded_source = source_pad(source)
    fine, left = smooth_section(potential, padded_source)
    cx, cy, cz = left.shape
    level_one = left.reshape(cx // 2, 2, cy // 2, 2, cz // 2, 2).sum(axis=(1, 3, 5)) * 0.5
    padded_one = source_pad(level_one)
    error_one = jnp.zeros_like(level_one)
    error_one, rest = smooth_section(error_one, padded_one)
    bx, by, bz = rest.shape
    local_block = jnp.sum(rest).reshape(1, 1, 1)
    gathered = lax.all_gather(local_block.reshape(1), ("gx", "gy", "gz"), axis=0, tiled=True)
    blocks = gathered.reshape(lax.axis_size("gx"), lax.axis_size("gy"), lax.axis_size("gz"))
    coarse = coarse_solve(blocks, float(by * bz), float(bx * bz), float(bx * by))
    own = coarse[lax.axis_index("gx"), lax.axis_index("gy"), lax.axis_index("gz")]
    error_one = error_one + own
    error_one, unused = smooth_section(error_one, padded_one)
    fine = fine + jnp.repeat(jnp.repeat(jnp.repeat(error_one, 2, 0), 2, 1), 2, 2)
    fine, unused = smooth_section(fine, padded_source)
    return fine


def solution(mesh):
    in_specs = (P("gx", "gy", "gz"), P("gx", "gy", "gz"))
    out_specs = P("gx", "gy", "gz")
    return jax.shard_map(body, mesh=mesh, in_specs=in_specs, out_specs=out_specs, check_vma=False)
```

profile of v0, /device:TPU:0, one launch (start us, length us, event | category | flops | bytes accessed | tf_op | source)
XLA Modules:
  0.0 207.3 jit_solution(16299900137311476484)
XLA Ops:
  0.0 3.0 %collective-permute-start.12 = (f32[5,8,64]{2,1,0:T(8,128)S(1)}, f32[5,8,64]{2,1,0:T(8,128)S(1)}, u32[]{:S(2)}, u32[]{:S(2)}) collective-permute-start(f32[5,8,64]{2,1,0:T(8,128)S(1)} %broadcast.505), channel_id=1, source_target_pairs={{0,16},{16,0},{1,17},{17,1},{2,18},{18,2},{3,19},{19,3},{4,20},{20... | collective-permute-start | bytes 30728 | tf_op jit(solution)/shard_map/ppermute | solution.py:16
  4.5 41.2 %psum.7 = f32[]{:T(128)} all-reduce(f32[]{:T(128)} %reduce_sum.27), channel_id=1, replica_groups=mesh['gx'=2,'gy'=4,'gz'=4] {'gx','gy','gz'}, use_global_device_ids=true, to_apply=%region_1.0 | all-reduce | flops 1 | bytes 8 | tf_op jit(solution)/shard_map/psum | solution.py:110
  47.3 2.5 %collective-permute-start.6 = (f32[4,16,128]{2,1,0:T(8,128)S(1)}, f32[4,16,128]{2,1,0:T(8,128)S(1)}, u32[]{:S(2)}, u32[]{:S(2)}) collective-permute-start(f32[4,16,128]{2,1,0:T(8,128)S(1)} %get-tuple-element.52), channel_id=1, source_target_pairs={{0,16},{16,0},{1,17},{17,1},{2,18},{18,2},{3,19},{19,3},{4,20},{20... | collective-permute-start | bytes 98312 | tf_op jit(solution)/shard_map/ppermute | solution.py:16
  54.9 2.3 %collective-permute-start.15 = (f32[16,5,64]{2,1,0:T(8,128)S(1)}, f32[16,5,64]{2,1,0:T(8,128)S(1)}, u32[]{:S(2)}, u32[]{:S(2)}) collective-permute-start(f32[16,5,64]{2,1,0:T(8,128)S(1)} %get-tuple-element.64), channel_id=1, source_target_pairs={{4,0},{8,4},{12,8},{0,12},{5,1},{9,5},{13,9},{1,13},{6,2},{10,6},{... | collective-permute-start | bytes 61448 | tf_op jit(solution)/shard_map/ppermute | solution.py:18
  57.4 3.8 %collective-permute-start.9 = (f32[20,4,128]{2,1,0:T(4,128)S(1)}, f32[20,4,128]{2,1,0:T(4,128)S(1)}, u32[]{:S(2)}, u32[]{:S(2)}) collective-permute-start(f32[20,4,128]{2,1,0:T(4,128)S(1)} %get-tuple-element.45), channel_id=1, source_target_pairs={{4,0},{8,4},{12,8},{0,12},{5,1},{9,5},{13,9},{1,13},{6,2},{10,6},{... | collective-permute-start | bytes 122888 | tf_op jit(solution)/shard_map/ppermute | solution.py:18
  63.4 2.7 %collective-permute-start.3 = (f32[22,5,128]{2,0,1:T(8,128)S(1)}, f32[22,5,128]{2,0,1:T(8,128)S(1)}, u32[]{:S(2)}, u32[]{:S(2)}) collective-permute-start(f32[22,5,128]{2,0,1:T(8,128)S(1)} %copy.206), channel_id=1, source_target_pairs={{4,0},{8,4},{12,8},{0,12},{5,1},{9,5},{13,9},{1,13},{6,2},{10,6},{... | collective-permute-start | bytes 168968 | tf_op jit(solution)/shard_map/ppermute | solution.py:18
  66.1 2.1 %collective-permute-done.2 = f32[22,5,128]{2,0,1:T(8,128)S(1)} collective-permute-done((f32[22,5,128]{2,0,1:T(8,128)S(1)}, f32[22,5,128]{2,0,1:T(8,128)S(1)}, u32[]{:S(2)}, u32[]{:S(2)}) %collective-permute-start.2) | collective-permute-done | bytes 56352 | tf_op jit(solution)/shard_map/ppermute | solution.py:16
  70.7 5.5 %collective-permute-done.4 = f32[22,26,5]{2,0,1:T(8,128)S(1)} collective-permute-done((f32[22,26,5]{2,0,1:T(8,128)S(1)}, f32[22,26,5]{2,0,1:T(8,128)S(1)}, u32[]{:S(2)}, u32[]{:S(2)}) %collective-permute-start.4) | collective-permute-done | bytes 11472 | tf_op jit(solution)/shard_map/ppermute | solution.py:16
  81.0 2.0 collective-permute-done.11
  87.1 7.7 %reshape.125 = f32[6,2,8,2,64,2]{5,4,3,2,1,0:T(8,128)} reshape(f32[12,16,128]{2,1,0:T(8,128)S(1)} %fusion.43) | data formatting | bytes 196608 | tf_op jit(solution)/shard_map/reshape | solution.py:115
  94.8 3.3 %reduce_sum.28 = f32[6,8,64]{2,1,0:T(8,128)S(1)} reduce(f32[6,2,8,2,64,2]{5,4,3,2,1,0:T(8,128)} %reshape.125, f32[]{:T(128)} %constant.271.clone.1), dimensions={1,3,5}, to_apply=%region_2.3 | reduce | flops 21504 | bytes 110596 | tf_op jit(solution)/shard_map/reduce_sum | solution.py:115
  98.1 2.1 collective-permute-start.18
  104.0 3.8 %collective-permute-start.21 = (f32[14,4,64]{2,1,0:T(4,128)S(1)}, f32[14,4,64]{2,1,0:T(4,128)S(1)}, u32[]{:S(2)}, u32[]{:S(2)}) collective-permute-start(f32[14,4,64]{2,1,0:T(4,128)S(1)} %get-tuple-element.66), channel_id=1, source_target_pairs={{4,0},{8,4},{12,8},{0,12},{5,1},{9,5},{13,9},{1,13},{6,2},{10,6},{... | collective-permute-start | bytes 43016 | tf_op jit(solution)/shard_map/ppermute | solution.py:18
  111.7 3.0 %collective-permute-done.16 = f32[16,18,5]{2,1,0:T(8,128)S(1)} collective-permute-done((f32[16,18,5]{2,1,0:T(8,128)S(1)}, f32[16,18,5]{2,1,0:T(8,128)S(1)}, u32[]{:S(2)}, u32[]{:S(2)}) %collective-permute-start.16) | collective-permute-done | bytes 5792 | tf_op jit(solution)/shard_map/ppermute | solution.py:16
  114.9 2.2 %collective-permute-done.22 = f32[14,16,4]{2,1,0:T(8,128)S(1)} collective-permute-done((f32[14,16,4]{2,1,0:T(8,128)S(1)}, f32[14,16,4]{2,1,0:T(8,128)S(1)}, u32[]{:S(2)}, u32[]{:S(2)}) %collective-permute-start.22) | collective-permute-done | bytes 3616 | tf_op jit(solution)/shard_map/ppermute | solution.py:16
  119.6 37.3 %all-reduce = f32[32]{0:T(128)S(1)} all-reduce(f32[32]{0:T(128)S(1)} %dynamic-update-slice), channel_id=1, replica_groups=mesh['gx'=2,'gy'=4,'gz'=4] {'gx','gy','gz'}, use_global_device_ids=true, to_apply=%add | all-reduce | flops 32 | bytes 256
  159.5 2.3 %collective-permute-start.24 = (f32[5,8,64]{2,1,0:T(8,128)S(1)}, f32[5,8,64]{2,1,0:T(8,128)S(1)}, u32[]{:S(2)}, u32[]{:S(2)}) collective-permute-start(f32[5,8,64]{2,1,0:T(8,128)S(1)} %get-tuple-element.67), channel_id=1, source_target_pairs={{0,16},{16,0},{1,17},{17,1},{2,18},{18,2},{3,19},{19,3},{4,20},{20... | collective-permute-start | bytes 30728 | tf_op jit(solution)/shard_map/ppermute | solution.py:16
  165.7 2.5 %collective-permute-start.26 = (f32[16,5,64]{2,1,0:T(8,128)S(1)}, f32[16,5,64]{2,1,0:T(8,128)S(1)}, u32[]{:S(2)}, u32[]{:S(2)}) collective-permute-start(f32[16,5,64]{2,1,0:T(8,128)S(1)} %get-tuple-element.61), channel_id=1, source_target_pairs={{0,4},{4,8},{8,12},{12,0},{1,5},{5,9},{9,13},{13,1},{2,6},{6,10},{... | collective-permute-start | bytes 61448 | tf_op jit(solution)/shard_map/ppermute | solution.py:16
  169.5 2.2 %collective-permute-done.26 = f32[16,5,64]{2,1,0:T(8,128)S(1)} collective-permute-done((f32[16,5,64]{2,1,0:T(8,128)S(1)}, f32[16,5,64]{2,1,0:T(8,128)S(1)}, u32[]{:S(2)}, u32[]{:S(2)}) %collective-permute-start.26) | collective-permute-done | bytes 20512 | tf_op jit(solution)/shard_map/ppermute | solution.py:16
  174.5 4.9 %collective-permute-done.28 = f32[16,18,5]{2,1,0:T(8,128)S(1)} collective-permute-done((f32[16,18,5]{2,1,0:T(8,128)S(1)}, f32[16,18,5]{2,1,0:T(8,128)S(1)}, u32[]{:S(2)}, u32[]{:S(2)}) %collective-permute-start.28) | collective-permute-done | bytes 5792 | tf_op jit(solution)/shard_map/ppermute | solution.py:16
  183.5 2.2 %collective-permute-done.30 = f32[5,16,128]{2,1,0:T(8,128)S(1)} collective-permute-done((f32[5,16,128]{2,1,0:T(8,128)S(1)}, f32[5,16,128]{2,1,0:T(8,128)S(1)}, u32[]{:S(2)}, u32[]{:S(2)}) %collective-permute-start.30) | collective-permute-done | bytes 40992 | tf_op jit(solution)/shard_map/ppermute | solution.py:16
  187.3 2.9 %collective-permute-start.33 = (f32[22,5,128]{2,0,1:T(8,128)S(1)}, f32[22,5,128]{2,0,1:T(8,128)S(1)}, u32[]{:S(2)}, u32[]{:S(2)}) collective-permute-start(f32[22,5,128]{2,0,1:T(8,128)S(1)} %copy.124), channel_id=1, source_target_pairs={{4,0},{8,4},{12,8},{0,12},{5,1},{9,5},{13,9},{1,13},{6,2},{10,6},{... | collective-permute-start | bytes 168968 | tf_op jit(solution)/shard_map/ppermute | solution.py:18
  190.2 2.5 %collective-permute-done.32 = f32[22,5,128]{2,0,1:T(8,128)S(1)} collective-permute-done((f32[22,5,128]{2,0,1:T(8,128)S(1)}, f32[22,5,128]{2,0,1:T(8,128)S(1)}, u32[]{:S(2)}, u32[]{:S(2)}) %collective-permute-start.32) | collective-permute-done | bytes 56352 | tf_op jit(solution)/shard_map/ppermute | solution.py:16
  195.0 6.5 %collective-permute-done.34 = f32[22,26,5]{2,0,1:T(8,128)S(1)} collective-permute-done((f32[22,26,5]{2,0,1:T(8,128)S(1)}, f32[22,26,5]{2,0,1:T(8,128)S(1)}, u32[]{:S(2)}, u32[]{:S(2)}) %collective-permute-start.34) | collective-permute-done | bytes 11472 | tf_op jit(solution)/shard_map/ppermute | solution.py:16
  (157 shorter events, 55.3 us)
Async XLA Ops:
  0.0 53.2 %collective-permute-start.12 = (f32[5,8,64]{2,1,0:T(8,128)S(1)}, f32[5,8,64]{2,1,0:T(8,128)S(1)}, u32[]{:S(2)}, u32[]{:S(2)}) collective-permute-start(f32[5,8,64]{2,1,0:T(8,128)S(1)} %broadcast.505), channel_id=1, source_target_pairs={{0,16},{16,0},{1,17},{17,1},{2,18},{18,2},{3,19},{19,3},{4,20},{20... | collective-permute-start | bytes 30728 | tf_op jit(solution)/shard_map/ppermute | solution.py:16
  4.5 48.8 %collective-permute-start.13 = (f32[5,8,64]{2,1,0:T(8,128)S(1)}, f32[5,8,64]{2,1,0:T(8,128)S(1)}, u32[]{:S(2)}, u32[]{:S(2)}) collective-permute-start(f32[5,8,64]{2,1,0:T(8,128)S(1)} %broadcast.505), channel_id=1, source_target_pairs={{16,0},{0,16},{17,1},{1,17},{18,2},{2,18},{19,3},{3,19},{20,4},{4,... | collective-permute-start | bytes 30728 | tf_op jit(solution)/shard_map/ppermute | solution.py:18
  47.3 7.7 %collective-permute-start.6 = (f32[4,16,128]{2,1,0:T(8,128)S(1)}, f32[4,16,128]{2,1,0:T(8,128)S(1)}, u32[]{:S(2)}, u32[]{:S(2)}) collective-permute-start(f32[4,16,128]{2,1,0:T(8,128)S(1)} %get-tuple-element.52), channel_id=1, source_target_pairs={{0,16},{16,0},{1,17},{17,1},{2,18},{18,2},{3,19},{19,3},{4,20},{20... | collective-permute-start | bytes 98312 | tf_op jit(solution)/shard_map/ppermute | solution.py:16
  49.8 7.5 %collective-permute-start.7 = (f32[4,16,128]{2,1,0:T(8,128)S(1)}, f32[4,16,128]{2,1,0:T(8,128)S(1)}, u32[]{:S(2)}, u32[]{:S(2)}) collective-permute-start(f32[4,16,128]{2,1,0:T(8,128)S(1)} %get-tuple-element.53), channel_id=1, source_target_pairs={{16,0},{0,16},{17,1},{1,17},{18,2},{2,18},{19,3},{3,19},{20,4},{4,... | collective-permute-start | bytes 98312 | tf_op jit(solution)/shard_map/ppermute | solution.py:18
  50.7 6.7 %collective-permute-start = (f32[5,16,128]{2,1,0:T(8,128)S(1)}, f32[5,16,128]{2,1,0:T(8,128)S(1)}, u32[]{:S(2)}, u32[]{:S(2)}) collective-permute-start(f32[5,16,128]{2,1,0:T(8,128)S(1)} %get-tuple-element.54), channel_id=1, source_target_pairs={{0,16},{16,0},{1,17},{17,1},{2,18},{18,2},{3,19},{19,3},{4,20},{20... | collective-permute-start | bytes 122888 | tf_op jit(solution)/shard_map/ppermute | solution.py:16
  53.2 8.0 %collective-permute-start.1 = (f32[5,16,128]{2,1,0:T(8,128)S(1)}, f32[5,16,128]{2,1,0:T(8,128)S(1)}, u32[]{:S(2)}, u32[]{:S(2)}) collective-permute-start(f32[5,16,128]{2,1,0:T(8,128)S(1)} %get-tuple-element.55), channel_id=1, source_target_pairs={{16,0},{0,16},{17,1},{1,17},{18,2},{2,18},{19,3},{3,19},{20,4},{4,... | collective-permute-start | bytes 122888 | tf_op jit(solution)/shard_map/ppermute | solution.py:18
  53.4 46.9 %collective-permute-start.14 = (f32[16,5,64]{2,1,0:T(8,128)S(1)}, f32[16,5,64]{2,1,0:T(8,128)S(1)}, u32[]{:S(2)}, u32[]{:S(2)}) collective-permute-start(f32[16,5,64]{2,1,0:T(8,128)S(1)} %get-tuple-element.63), channel_id=1, source_target_pairs={{0,4},{4,8},{8,12},{12,0},{1,5},{5,9},{9,13},{13,1},{2,6},{6,10},{... | collective-permute-start | bytes 61448 | tf_op jit(solution)/shard_map/ppermute | solution.py:16
  54.9 45.3 %collective-permute-start.15 = (f32[16,5,64]{2,1,0:T(8,128)S(1)}, f32[16,5,64]{2,1,0:T(8,128)S(1)}, u32[]{:S(2)}, u32[]{:S(2)}) collective-permute-start(f32[16,5,64]{2,1,0:T(8,128)S(1)} %get-tuple-element.64), channel_id=1, source_target_pairs={{4,0},{8,4},{12,8},{0,12},{5,1},{9,5},{13,9},{1,13},{6,2},{10,6},{... | collective-permute-start | bytes 61448 | tf_op jit(solution)/shard_map/ppermute | solution.py:18
  57.4 8.7 %collective-permute-start.9 = (f32[20,4,128]{2,1,0:T(4,128)S(1)}, f32[20,4,128]{2,1,0:T(4,128)S(1)}, u32[]{:S(2)}, u32[]{:S(2)}) collective-permute-start(f32[20,4,128]{2,1,0:T(4,128)S(1)} %get-tuple-element.45), channel_id=1, source_target_pairs={{4,0},{8,4},{12,8},{0,12},{5,1},{9,5},{13,9},{1,13},{6,2},{10,6},{... | collective-permute-start | bytes 122888 | tf_op jit(solution)/shard_map/ppermute | solution.py:18
  62.1 6.1 %collective-permute-start.2 = (f32[22,5,128]{2,0,1:T(8,128)S(1)}, f32[22,5,128]{2,0,1:T(8,128)S(1)}, u32[]{:S(2)}, u32[]{:S(2)}) collective-permute-start(f32[22,5,128]{2,0,1:T(8,128)S(1)} %copy.205), channel_id=1, source_target_pairs={{0,4},{4,8},{8,12},{12,0},{1,5},{5,9},{9,13},{13,1},{2,6},{6,10},{... | collective-permute-start | bytes 168968 | tf_op jit(solution)/shard_map/ppermute | solution.py:16
  68.5 7.7 %collective-permute-start.4 = (f32[22,26,5]{2,0,1:T(8,128)S(1)}, f32[22,26,5]{2,0,1:T(8,128)S(1)}, u32[]{:S(2)}, u32[]{:S(2)}) collective-permute-start(f32[22,26,5]{2,0,1:T(8,128)S(1)} %get-tuple-element.32), channel_id=1, source_target_pairs={{0,1},{1,2},{2,3},{3,0},{4,5},{5,6},{6,7},{7,4},{8,9},{9,10},{10,1... | collective-permute-start | bytes 34328 | tf_op jit(solution)/shard_map/ppermute | solution.py:16
  68.6 9.7 %collective-permute-start.5 = (f32[22,26,5]{2,0,1:T(8,128)S(1)}, f32[22,26,5]{2,0,1:T(8,128)S(1)}, u32[]{:S(2)}, u32[]{:S(2)}) collective-permute-start(f32[22,26,5]{2,0,1:T(8,128)S(1)} %get-tuple-element.33), channel_id=1, source_target_pairs={{1,0},{2,1},{3,2},{0,3},{5,4},{6,5},{7,6},{4,7},{9,8},{10,9},{11,1... | collective-permute-start | bytes 34328 | tf_op jit(solution)/shard_map/ppermute | solution.py:18
  70.4 10.6 %collective-permute-start.10 = (f32[20,24,4]{2,1,0:T(8,128)S(1)}, f32[20,24,4]{2,1,0:T(8,128)S(1)}, u32[]{:S(2)}, u32[]{:S(2)}) collective-permute-start(f32[20,24,4]{2,1,0:T(8,128)S(1)} %get-tuple-element.34), channel_id=1, source_target_pairs={{0,1},{1,2},{2,3},{3,0},{4,5},{5,6},{6,7},{7,4},{8,9},{9,10},{10,1... | collective-permute-start | bytes 23048 | tf_op jit(solution)/shard_map/ppermute | solution.py:16
  76.2 6.9 %collective-permute-start.11 = (f32[20,24,4]{2,1,0:T(8,128)S(1)}, f32[20,24,4]{2,1,0:T(8,128)S(1)}, u32[]{:S(2)}, u32[]{:S(2)}) collective-permute-start(f32[20,24,4]{2,1,0:T(8,128)S(1)} %get-tuple-element.35), channel_id=1, source_target_pairs={{1,0},{2,1},{3,2},{0,3},{5,4},{6,5},{7,6},{4,7},{9,8},{10,9},{11,1... | collective-permute-start | bytes 23048 | tf_op jit(solution)/shard_map/ppermute | solution.py:18
  107.9 6.7 %collective-permute-start.16 = (f32[16,18,5]{2,1,0:T(8,128)S(1)}, f32[16,18,5]{2,1,0:T(8,128)S(1)}, u32[]{:S(2)}, u32[]{:S(2)}) collective-permute-start(f32[16,18,5]{2,1,0:T(8,128)S(1)} %get-tuple-element.38), channel_id=1, source_target_pairs={{0,1},{1,2},{2,3},{3,0},{4,5},{5,6},{6,7},{7,4},{8,9},{9,10},{10,1... | collective-permute-start | bytes 17288 | tf_op jit(solution)/shard_map/ppermute | solution.py:16
  108.0 6.7 %collective-permute-start.17 = (f32[16,18,5]{2,1,0:T(8,128)S(1)}, f32[16,18,5]{2,1,0:T(8,128)S(1)}, u32[]{:S(2)}, u32[]{:S(2)}) collective-permute-start(f32[16,18,5]{2,1,0:T(8,128)S(1)} %get-tuple-element.39), channel_id=1, source_target_pairs={{1,0},{2,1},{3,2},{0,3},{5,4},{6,5},{7,6},{4,7},{9,8},{10,9},{11,1... | collective-permute-start | bytes 17288 | tf_op jit(solution)/shard_map/ppermute | solution.py:18
  109.9 7.2 %collective-permute-start.22 = (f32[14,16,4]{2,1,0:T(8,128)S(1)}, f32[14,16,4]{2,1,0:T(8,128)S(1)}, u32[]{:S(2)}, u32[]{:S(2)}) collective-permute-start(f32[14,16,4]{2,1,0:T(8,128)S(1)} %get-tuple-element.48), channel_id=1, source_target_pairs={{0,1},{1,2},{2,3},{3,0},{4,5},{5,6},{6,7},{7,4},{8,9},{9,10},{10,1... | collective-permute-start | bytes 10760 | tf_op jit(solution)/shard_map/ppermute | solution.py:16
  109.9 7.2 %collective-permute-start.23 = (f32[14,16,4]{2,1,0:T(8,128)S(1)}, f32[14,16,4]{2,1,0:T(8,128)S(1)}, u32[]{:S(2)}, u32[]{:S(2)}) collective-permute-start(f32[14,16,4]{2,1,0:T(8,128)S(1)} %get-tuple-element.49), channel_id=1, source_target_pairs={{1,0},{2,1},{3,2},{0,3},{5,4},{6,5},{7,6},{4,7},{9,8},{10,9},{11,1... | collective-permute-start | bytes 10760 | tf_op jit(solution)/shard_map/ppermute | solution.py:18
  165.7 6.1 %collective-permute-start.26 = (f32[16,5,64]{2,1,0:T(8,128)S(1)}, f32[16,5,64]{2,1,0:T(8,128)S(1)}, u32[]{:S(2)}, u32[]{:S(2)}) collective-permute-start(f32[16,5,64]{2,1,0:T(8,128)S(1)} %get-tuple-element.61), channel_id=1, source_target_pairs={{0,4},{4,8},{8,12},{12,0},{1,5},{5,9},{9,13},{13,1},{2,6},{6,10},{... | collective-permute-start | bytes 61448 | tf_op jit(solution)/shard_map/ppermute | solution.py:16
  172.6 6.7 %collective-permute-start.28 = (f32[16,18,5]{2,1,0:T(8,128)S(1)}, f32[16,18,5]{2,1,0:T(8,128)S(1)}, u32[]{:S(2)}, u32[]{:S(2)}) collective-permute-start(f32[16,18,5]{2,1,0:T(8,128)S(1)} %get-tuple-element.36), channel_id=1, source_target_pairs={{0,1},{1,2},{2,3},{3,0},{4,5},{5,6},{6,7},{7,4},{8,9},{9,10},{10,1... | collective-permute-start | bytes 17288 | tf_op jit(solution)/shard_map/ppermute | solution.py:16
  172.7 6.6 %collective-permute-start.29 = (f32[16,18,5]{2,1,0:T(8,128)S(1)}, f32[16,18,5]{2,1,0:T(8,128)S(1)}, u32[]{:S(2)}, u32[]{:S(2)}) collective-permute-start(f32[16,18,5]{2,1,0:T(8,128)S(1)} %get-tuple-element.37), channel_id=1, source_target_pairs={{1,0},{2,1},{3,2},{0,3},{5,4},{6,5},{7,6},{4,7},{9,8},{10,9},{11,1... | collective-permute-start | bytes 17288 | tf_op jit(solution)/shard_map/ppermute | solution.py:18
  186.3 6.5 %collective-permute-start.32 = (f32[22,5,128]{2,0,1:T(8,128)S(1)}, f32[22,5,128]{2,0,1:T(8,128)S(1)}, u32[]{:S(2)}, u32[]{:S(2)}) collective-permute-start(f32[22,5,128]{2,0,1:T(8,128)S(1)} %copy.123), channel_id=1, source_target_pairs={{0,4},{4,8},{8,12},{12,0},{1,5},{5,9},{9,13},{13,1},{2,6},{6,10},{... | collective-permute-start | bytes 168968 | tf_op jit(solution)/shard_map/ppermute | solution.py:16
  193.0 8.5 %collective-permute-start.34 = (f32[22,26,5]{2,0,1:T(8,128)S(1)}, f32[22,26,5]{2,0,1:T(8,128)S(1)}, u32[]{:S(2)}, u32[]{:S(2)}) collective-permute-start(f32[22,26,5]{2,0,1:T(8,128)S(1)} %get-tuple-element.30), channel_id=1, source_target_pairs={{0,1},{1,2},{2,3},{3,0},{4,5},{5,6},{6,7},{7,4},{8,9},{9,10},{10,1... | collective-permute-start | bytes 34328 | tf_op jit(solution)/shard_map/ppermute | solution.py:16
  193.0 8.4 %collective-permute-start.35 = (f32[22,26,5]{2,0,1:T(8,128)S(1)}, f32[22,26,5]{2,0,1:T(8,128)S(1)}, u32[]{:S(2)}, u32[]{:S(2)}) collective-permute-start(f32[22,26,5]{2,0,1:T(8,128)S(1)} %get-tuple-element.31), channel_id=1, source_target_pairs={{1,0},{2,1},{3,2},{0,3},{5,4},{6,5},{7,6},{4,7},{9,8},{10,9},{11,1... | collective-permute-start | bytes 34328 | tf_op jit(solution)/shard_map/ppermute | solution.py:18
  (13 other events, 59.1 us)
where the time goes:
time: 208 us; the launch traced here: 207 us
  blocking collectives  78.5 us (38%)
  waiting for transfers between devices  46.4 us (22%)
  starting transfers between devices  45.8 us (22%)
  other arithmetic  20.5 us (10%)
  local copies, waits for them, and re-layouts  13.7 us (7%)
    psum x1, blocking collectives, body(): total = lax.psum(jnp.sum(density), ('gx', 'gy', 'gz'))  41.2 us
    unnamed x1, blocking collectives  37.3 us
    ppermute x18, waiting for transfers between devices, with_halo(): lax.ppermute(tail, axis, [(i, (i + 1) % count) for i in range(count)])  37.1 us
    ppermute x18, starting transfers between devices, with_halo(): lax.ppermute(head, axis, [((i + 1) % count, i) for i in range(count)])  27.9 us
    ppermute x18, starting transfers between devices, with_halo(): lax.ppermute(tail, axis, [(i, (i + 1) % count) for i in range(count)])  17.9 us
    ppermute x18, waiting for transfers between devices, with_halo(): lax.ppermute(head, axis, [((i + 1) % count, i) for i in range(count)])  9.25 us
    reshape x1, local copies, waits for them, and re-layouts, body(): left.reshape(cx // 2, 2, cy // 2, 2, cz // 2, 2).sum(axis=(1, 3, 5)) * 0.5  7.66 us
    select_n x8, other arithmetic, sectioned(): jnp.where(red_shell, (inner_sum(current) - trim(padded_source, reach - de...  5.3 us
  transfers between devices with their start and end apart: 36, of which 19 were waited for; matrix products, arithmetic and copies ran while one was open for 11% of the time, Pallas kernels for 0%

commit v1 on v0

v1 whole, which is shorter than its diff:
```python
import functools
import numpy as np
import jax
import jax.numpy as jnp
from jax import lax
from jax.experimental import pallas as pl
from jax.experimental.pallas import tpu as pltpu
from jax.sharding import PartitionSpec as P

SWEEPS = 2
HI = lax.Precision.HIGHEST
MESH = pl.DeviceIdType.MESH
R = 8


def table(count):
    modes = (np.arange(count) + 1) // 2
    angle = 2 * np.pi * np.outer(np.arange(count), modes) / count
    q = np.where(np.arange(count) % 2 == 1, np.cos(angle), np.sin(angle)) * np.sqrt(2 / count)
    q = np.where(2 * modes == count, np.cos(angle) / np.sqrt(count), q)
    q[:, 0] = 1 / np.sqrt(count)
    return q, 2 - 2 * np.cos(2 * np.pi * modes / count)


def coarse_operator(nx, ny, nz, wx, wy, wz):
    qx, lx = table(nx)
    qy, ly = table(ny)
    qz, lz = table(nz)
    q = np.kron(np.kron(qx, qy), qz)
    lam = wx * lx[:, None, None] + wy * ly[None, :, None] + wz * lz[None, None, :]
    lam = lam.reshape(-1)
    inv = np.concatenate([[0.0], -1.0 / lam[1:]])
    return ((q * inv) @ q.T).astype(np.float32)


def kernel(
    dims, den_hbm, pot_hbm, op_ref, sz_ref, sy_ref, rz_ref, ry_ref, out_ref,
    pa, pb, den, lv, ea, eb, e2, f2, gat, cv,
    pk_p, pk_d, pk_l, pk_e, pk_f, rk_p, rk_d, rk_l, rk_e, rk_f,
    ssem, rsem, gs, gr, lsem,
):
    nx, ny, nz, X, Y, Z = dims
    n = nx * ny * nz
    x1, y1, z1 = X // 2, Y // 2, Z // 2
    ix, iy, iz = lax.axis_index("gx"), lax.axis_index("gy"), lax.axis_index("gz")
    me = (ix * ny + iy) * nz + iz

    def device(o):
        ox, oy, oz = o // (ny * nz), (o // nz) % ny, o % nz
        return (lax.rem(ix + ox, nx), lax.rem(iy + oy, ny), lax.rem(iz + oz, nz))

    load_p = pltpu.make_async_copy(pot_hbm, pa.at[pl.ds(5, X), pl.ds(R, Y), pl.ds(0, Z)], lsem.at[0])
    load_d = pltpu.make_async_copy(den_hbm, den.at[pl.ds(5, X), pl.ds(R, Y), pl.ds(0, Z)], lsem.at[1])
    load_p.start()
    load_d.start()

    barrier = pltpu.get_barrier_semaphore()

    def greet(o, carry):
        pl.semaphore_signal(barrier, inc=1, device_id=device(o), device_id_type=MESH)
        return carry

    lax.fori_loop(1, n, greet, 0)
    pl.semaphore_wait(barrier, n - 1)
    load_p.wait()
    load_d.wait()

    sems = iter(range(60))

    def send(src, dst, step):
        k = next(sems)
        to = {
            0: (lax.rem(ix + step + nx, nx), iy, iz),
            1: (ix, lax.rem(iy + step + ny, ny), iz),
            2: (ix, iy, lax.rem(iz + step + nz, nz)),
        }[send.axis]
        copy = pltpu.make_async_remote_copy(
            src_ref=src, dst_ref=dst, send_sem=ssem.at[k], recv_sem=rsem.at[k],
            device_id=to, device_id_type=MESH,
        )
        copy.start()
        return copy

    def exchange(items):
        send.axis = 0
        copies = []
        for buf, h, H, (sx, sy, sz), pk, rk in items:
            rows, lanes = pl.ds(R, sy), pl.ds(0, 128)
            copies.append(send(buf.at[pl.ds(H + sx - h, h), rows, lanes], buf.at[pl.ds(H - h, h), rows, lanes], 1))
            copies.append(send(buf.at[pl.ds(H, h), rows, lanes], buf.at[pl.ds(H + sx, h), rows, lanes], -1))
        for copy in copies:
            copy.wait()
        send.axis = 1
        copies = []
        for buf, h, H, (sx, sy, sz), pk, rk in items:
            planes, lanes = pl.ds(H - h, sx + 2 * h), pl.ds(0, 128)
            copies.append(send(buf.at[planes, pl.ds(sy, R), lanes], buf.at[planes, pl.ds(0, R), lanes], 1))
            copies.append(send(buf.at[planes, pl.ds(R, R), lanes], buf.at[planes, pl.ds(R + sy, R), lanes], -1))
        for copy in copies:
            copy.wait()
        send.axis = 2
        copies = []
        for buf, h, H, (sx, sy, sz), pk, rk in items:
            rows = sy + 2 * R
            lane = lax.broadcasted_iota(jnp.int32, (rows, 128), 1)
            head = tail = jnp.zeros((rows, 128), jnp.float32)
            for q in range(sx + 2 * h):
                v = buf[H - h + q, :, 0:128]
                inside = (lane >= q * h) & (lane < q * h + h)
                tail = jnp.where(inside, pltpu.roll(v, (q * h - (sz - h)) % 128, 1), tail)
                head = jnp.where(inside, pltpu.roll(v, q * h, 1) if q else v, head)
            pk[0] = tail
            pk[1] = head
            copies.append(send(pk.at[0], rk.at[0], 1))
            copies.append(send(pk.at[1], rk.at[1], -1))
        for copy in copies:
            copy.wait()
        for buf, h, H, (sx, sy, sz), pk, rk in items:
            rows = sy + 2 * R
            lane = lax.broadcasted_iota(jnp.int32, (rows, 128), 1)
            left, right = rk[0], rk[1]
            wide = sz == 128
            at = 0 if wide else sz
            for q in range(sx + 2 * h):
                a = pltpu.roll(left, (128 - h - q * h) % 128, 1)
                b = pltpu.roll(right, (at - q * h) % 128, 1)
                edge = jnp.where(lane >= 112, a, b)
                if wide:
                    buf[H - h + q, :, 128:256] = edge
                else:
                    buf[H - h + q] = jnp.where(lane < sz, buf[H - h + q], edge)

    sixth = jnp.float32(1.0 / 6.0)

    def masks(rows, lanes):
        even = (
            lax.broadcasted_iota(jnp.int32, (rows, lanes), 0)
            + lax.broadcasted_iota(jnp.int32, (rows, lanes), 1)
        ) % 2 == 0
        return even, jnp.logical_not(even)

    def beside(a, p, c):
        rows, lanes = c.shape
        t = a[p - 1] + a[p + 1]
        t = t + (pltpu.roll(c, 1, 0) + pltpu.roll(c, rows - 1, 0))
        return t + (pltpu.roll(c, 1, 1) + pltpu.roll(c, lanes - 1, 1))

    def half(a, b, s, lo, hi, H, off, colour, mask, shift=None):
        for p in range(lo, hi):
            c = a[p]
            t = beside(a, p, c) - s[p + off]
            if shift is not None:
                t = t + shift
            b[p] = jnp.where(mask[(p - H + colour) % 2], t * sixth, c)

    fine_mask = masks(Y + 2 * R, 2 * Z)
    one_mask = masks(y1 + 2 * R, 128)

    exchange([(pa, 5, 5, (X, Y, Z), pk_p, rk_p), (den, 4, 5, (X, Y, Z), pk_d, rk_d)])
    for k, (a, b) in enumerate(((pa, pb), (pb, pa), (pa, pb), (pb, pa))):
        d = 4 - k
        half(a, b, den, 5 - d, 5 + X + d, 5, 0, k % 2, fine_mask)
    pairs = []
    total = jnp.zeros((Y, Z), jnp.float32)
    for q in range(x1):
        both = None
        for p in (5 + 2 * q, 6 + 2 * q):
            c = pa[p]
            left = (den[p] - (beside(pa, p, c) - 6.0 * c))[R : R + Y, 0:Z]
            both = left if both is None else both + left
            total = total + den[p, R : R + Y, 0:Z]
            f2[p - 1, R : R + Y, 0:Z] = c[R : R + Y, 0:Z]
        pairs.append(both)
    stacked = jnp.concatenate(pairs, axis=0)
    stacked = jnp.dot(stacked, sz_ref[...], precision=HI, preferred_element_type=jnp.float32)
    one = jnp.dot(sy_ref[...], stacked, precision=HI, preferred_element_type=jnp.float32) * 0.5
    for q in range(x1):
        lv[6 + q, R : R + y1, :] = one[q * y1 : (q + 1) * y1]

    exchange([(lv, 5, 6, (x1, y1, z1), pk_l, rk_l)])
    for p in range(6 - 4, 6 + x1 + 4):
        ea[p] = jnp.where(one_mask[p % 2], lv[p] * -sixth, 0.0)
    for k, (a, b) in enumerate(((ea, eb), (eb, ea), (ea, eb))):
        d = 3 - k
        half(a, b, lv, 6 - d, 6 + x1 + d, 6, 0, (k + 1) % 2, one_mask)
    acc = jnp.zeros((y1, 128), jnp.float32)
    for p in range(6, 6 + x1):
        c = eb[p]
        e2[p, R : R + y1, :] = c[R : R + y1]
        acc = acc + (lv[p] - (beside(eb, p, c) - 6.0 * c))[R : R + y1]
    lane = lax.broadcasted_iota(jnp.int32, (y1, 128), 1)
    acc = jnp.where(lane < z1, acc, 0.0)

    def whole_sum(v):
        return jnp.sum(jnp.sum(v, axis=0, keepdims=True), axis=1, keepdims=True)

    gat[me, :, 0:128] = jnp.broadcast_to(whole_sum(acc), (1, 128))
    gat[me, :, 128:256] = jnp.broadcast_to(whole_sum(total), (1, 128))

    def spread(o, carry):
        pltpu.make_async_remote_copy(
            src_ref=gat.at[me], dst_ref=gat.at[me], send_sem=gs, recv_sem=gr,
            device_id=device(o), device_id_type=MESH,
        ).start()
        return carry

    lax.fori_loop(1, n, spread, 0)
    exchange([(e2, 6, 6, (x1, y1, z1), pk_e, rk_e), (f2, 4, 4, (X, Y, Z), pk_f, rk_f)])
    others = gat.at[pl.ds(0, n - 1)]
    pltpu.make_async_copy(others, others, gs).wait()
    pltpu.make_async_copy(others, others, gr).wait()

    values = gat[:, 0, :]
    blocks = values[:, 0:128]
    mean = jnp.sum(values[:, 128:256], axis=0, keepdims=True) / jnp.float32(n * X * Y * Z)
    blocks = blocks - jnp.sum(blocks, axis=0, keepdims=True) / jnp.float32(n)
    cv[...] = jnp.dot(op_ref[...], blocks, precision=HI, preferred_element_type=jnp.float32)
    row = lax.broadcasted_iota(jnp.int32, (y1 + 2 * R, 128), 0)
    lane = lax.broadcasted_iota(jnp.int32, (y1 + 2 * R, 128), 1)
    maps = []
    for dx in (-1, 0, 1):
        by_row = []
        for dy in (-1, 0, 1):
            vals = []
            for dz in (-1, 0, 1):
                at = (lax.rem(ix + dx + nx, nx) * ny + lax.rem(iy + dy + ny, ny)) * nz
                vals.append(cv[pl.ds(at + lax.rem(iz + dz + nz, nz), 1), :])
            by_row.append(jnp.where(lane < z1, vals[1], jnp.where(lane < (z1 + 128) // 2, vals[2], vals[0])))
        maps.append(jnp.where(row < R, by_row[0], jnp.where(row < R + y1, by_row[1], by_row[2])))
    for p in range(0, x1 + 12):
        which = 0 if p < 6 else (1 if p < 6 + x1 else 2)
        ea[p] = e2[p] + (maps[which] + mean * jnp.float32(8.0 / 3.0))
    for k, (a, b) in enumerate(((ea, eb), (eb, ea), (ea, eb), (eb, ea))):
        d = 5 - k
        half(a, b, lv, 6 - d, 6 + x1 + d, 6, 0, k % 2, one_mask, 4.0 * mean)

    mean2 = jnp.concatenate([mean, mean], axis=1)
    for q in range(4, 6 + x1 + 2):
        wide = jnp.dot(ea[q], rz_ref[...], precision=HI, preferred_element_type=jnp.float32)
        wide = jnp.dot(ry_ref[...], wide, precision=HI, preferred_element_type=jnp.float32)
        wide = wide + mean2 * jnp.float32(2.0 / 3.0)
        for p in (2 * (q - 4), 2 * (q - 4) + 1):
            pb[p] = f2[p] + wide
    for k, (a, b) in enumerate(((pb, pa), (pa, pb), (pb, pa))):
        d = 3 - k
        half(a, b, den, 4 - d, 4 + X + d, 4, 1, k % 2, fine_mask, mean2)
    for p in range(4, 4 + X):
        c = pa[p]
        t = (beside(pa, p, c) - den[p + 1] + mean2) * sixth
        out_ref[p - 4] = jnp.where(fine_mask[(p - 3) % 2], t, c)[R : R + Y, 0:Z]


def body(dims, density, potential):
    nx, ny, nz, X, Y, Z = dims
    n = nx * ny * nz
    x1, y1, z1 = X // 2, Y // 2, Z // 2
    op = coarse_operator(nx, ny, nz, float(y1 * z1), float(x1 * z1), float(x1 * y1))
    sz = (np.arange(Z)[:, None] // 2 == np.arange(128)[None, :]).astype(np.float32)
    r = np.arange(x1 * y1)
    c = np.arange(x1 * Y)
    sy = (r[:, None] == c[None, :] // 2).astype(np.float32)
    rz = (np.arange(128)[:, None] == np.arange(2 * Z)[None, :] // 2).astype(np.float32)
    rows, rows1 = Y + 2 * R, y1 + 2 * R
    ry = (np.arange(rows)[:, None] // 2 + R // 2 == np.arange(rows1)[None, :]).astype(np.float32)
    f32 = jnp.float32
    fine, one = (rows, 128), (rows1, 128)
    vmem = pl.BlockSpec(memory_space=pltpu.VMEM)
    return pl.pallas_call(
        functools.partial(kernel, dims),
        out_shape=jax.ShapeDtypeStruct((X, Y, Z), f32),
        in_specs=[pl.BlockSpec(memory_space=pl.ANY)] * 2 + [vmem] * 5,
        out_specs=vmem,
        scratch_shapes=[
            pltpu.VMEM((X + 10, rows, 2 * Z), f32),
            pltpu.VMEM((X + 10, rows, 2 * Z), f32),
            pltpu.VMEM((X + 10, rows, 2 * Z), f32),
            pltpu.VMEM((x1 + 12, rows1, 128), f32),
            pltpu.VMEM((x1 + 12, rows1, 128), f32),
            pltpu.VMEM((x1 + 12, rows1, 128), f32),
            pltpu.VMEM((x1 + 12, rows1, 128), f32),
            pltpu.VMEM((X + 8, rows, 2 * Z), f32),
            pltpu.VMEM((n, 1, 256), f32),
            pltpu.VMEM((n, 128), f32),
        ]
        + [pltpu.VMEM((2,) + s, f32) for s in (fine, fine, one, one, fine)] * 2
        + [
            pltpu.SemaphoreType.DMA((40,)),
            pltpu.SemaphoreType.DMA((40,)),
            pltpu.SemaphoreType.DMA,
            pltpu.SemaphoreType.DMA,
            pltpu.SemaphoreType.DMA((2,)),
        ],
        compiler_params=pltpu.CompilerParams(collective_id=0, has_side_effects=True),
        name="vcycle",
    )(density, potential, op, sz, sy, rz, ry)


def solution(mesh):
    nx, ny, nz = (mesh.shape[a] for a in ("gx", "gy", "gz"))

    def run(density, potential):
        return body((nx, ny, nz) + density.shape, density, potential)

    spec = P("gx", "gy", "gz")
    return jax.shard_map(run, mesh=mesh, in_specs=(spec, spec), out_specs=spec, check_vma=False)
```

time: 208 us -> 59.7 us (0.29)
  blocking collectives: 78.5 us -> 0 us
  Pallas kernels: 0 us -> 57.8 us
  waiting for transfers between devices: 46.4 us -> 0 us
  starting transfers between devices: 45.8 us -> 0 us
  other arithmetic: 20.5 us -> 0 us
  local copies, waits for them, and re-layouts: 13.7 us -> 1.54 us
    pallas_call x0 -> x1, Pallas kernels: none -> 57.8 us  [body(): pl.pallas_call(functools.partial(kernel, dims), out_shape=jax.ShapeDtypeS...]
    ppermute x36 -> x0, waiting for transfers between devices: 46.4 us -> none  [the longest x18 37.1 us: with_halo(): lax.ppermute(tail, axis, [(i, (i + 1) % count) for i in range(count)])]
    ppermute x36 -> x0, starting transfers between devices: 45.8 us -> none  [the longest x18 27.9 us: with_halo(): lax.ppermute(head, axis, [((i + 1) % count, i) for i in range(count)])]
    psum x1 -> x0, blocking collectives: 41.2 us -> none  [body(): total = lax.psum(jnp.sum(density), ('gx', 'gy', 'gz'))]
    unnamed x1 -> x0, blocking collectives: 37.3 us -> none
    select_n x16 -> x0, other arithmetic: 8.79 us -> none  [the longest x8 5.3 us: sectioned(): jnp.where(red_shell, (inner_sum(current) - trim(padded_source, reach - de...]
    reshape x5 -> x0, local copies, waits for them, and re-layouts: 8.24 us -> none  [the longest x1 7.66 us: body(): left.reshape(cx // 2, 2, cy // 2, 2, cz // 2, 2).sum(axis=(1, 3, 5)) * 0.5]
    reduce_sum x3 -> x0, other arithmetic: 5.51 us -> none  [the longest x1 3.28 us: body(): left.reshape(cx // 2, 2, cy // 2, 2, cz // 2, 2).sum(axis=(1, 3, 5)) * 0.5]
  transfers between devices with their start and end apart: 36 -> 0, of which waited for: 19 -> 0; matrix products, arithmetic and copies ran while one was open for 11% -> 0% of each run, Pallas kernels for 0% -> 0%
where the time goes in v1:
time: 59.7 us; the launch traced here: 59.3 us
  Pallas kernels  57.8 us (97%)
  local copies, waits for them, and re-layouts  1.54 us (3%)
    pallas_call x1, Pallas kernels, body(): pl.pallas_call(functools.partial(kernel, dims), out_shape=jax.ShapeDtypeS...  57.8 us
    unnamed x1, local copies, waits for them, and re-layouts  1.54 us

profile of v1, /device:TPU:0, one launch (start us, length us, event | category | flops | bytes accessed | tf_op | source)
XLA Modules:
  0.0 59.3 jit_solution(3376849608497012708)
XLA Ops:
  0.0 57.8 %vcycle.1 = f32[12,16,128]{2,1,0:T(8,128)} custom-call(f32[12,16,128]{2,1,0:T(8,128)} %den_hbm.1, f32[12,16,128]{2,1,0:T(8,128)} %pot_hbm.1, f32[32,32]{1,0:T(8,128)} %constant.10.clone.op_ref, f32[128,128]{1,0:T(8,128)} %constant.11.clone.sz_ref, f32[48,96]{1,0:T(8,128)} %constant.12.clone.sy_ref, f32[128,256]{1,0:T(8,128)} %constant.13.clone.rz_ref, ...), custom_call_target="tpu_custom_call" | custom-call | tf_op jit(solution)/shard_map/vcycle/pallas_call | solution.py:268
  57.8 1.5 %copy.9 = f32[12,16,128]{2,1,0:T(8,128)} copy(f32[12,16,128]{2,1,0:T(8,128)} %vcycle.1) | data formatting | bytes 196608

commit v2 on v1

v2 whole, which is shorter than its diff:
```python
import functools
import numpy as np
import jax
import jax.numpy as jnp
from jax import lax
from jax.experimental import pallas as pl
from jax.experimental.pallas import tpu as pltpu
from jax.sharding import PartitionSpec as P

SWEEPS = 2
HI = lax.Precision.HIGHEST
MESH = pl.DeviceIdType.MESH
R = 8


def table(count):
    modes = (np.arange(count) + 1) // 2
    angle = 2 * np.pi * np.outer(np.arange(count), modes) / count
    q = np.where(np.arange(count) % 2 == 1, np.cos(angle), np.sin(angle)) * np.sqrt(2 / count)
    q = np.where(2 * modes == count, np.cos(angle) / np.sqrt(count), q)
    q[:, 0] = 1 / np.sqrt(count)
    return q, 2 - 2 * np.cos(2 * np.pi * modes / count)


def coarse_operator(nx, ny, nz, wx, wy, wz):
    qx, lx = table(nx)
    qy, ly = table(ny)
    qz, lz = table(nz)
    q = np.kron(np.kron(qx, qy), qz)
    lam = wx * lx[:, None, None] + wy * ly[None, :, None] + wz * lz[None, None, :]
    lam = lam.reshape(-1)
    inv = np.concatenate([[0.0], -1.0 / lam[1:]])
    return ((q * inv) @ q.T).astype(np.float32)


def kernel(
    dims, den_hbm, pot_hbm, op_ref, sz_ref, sy_ref, rz_ref, ry_ref, out_ref,
    own, pm, pa, pb, den, lv, ea, eb, e2, f2, gat, cv,
    pk_p, pk_l, pk_e, pk_f, rk_p, rk_l, rk_e, rk_f,
    ssem, rsem, gs, gr, lsem,
):
    nx, ny, nz, X, Y, Z = dims
    n = nx * ny * nz
    x1, y1, z1 = X // 2, Y // 2, Z // 2
    ix, iy, iz = lax.axis_index("gx"), lax.axis_index("gy"), lax.axis_index("gz")
    me = (ix * ny + iy) * nz + iz

    def device(o):
        ox, oy, oz = o // (ny * nz), (o // nz) % ny, o % nz
        return (lax.rem(ix + ox, nx), lax.rem(iy + oy, ny), lax.rem(iz + oz, nz))

    load_p = pltpu.make_async_copy(pot_hbm, own, lsem.at[0])
    load_d = pltpu.make_async_copy(den_hbm, den.at[pl.ds(6, X), pl.ds(R, Y), pl.ds(0, Z)], lsem.at[1])
    load_p.start()
    load_d.start()

    barrier = pltpu.get_barrier_semaphore()

    def greet(o, carry):
        pl.semaphore_signal(barrier, inc=1, device_id=device(o), device_id_type=MESH)
        return carry

    lax.fori_loop(1, n, greet, 0)
    load_p.wait()
    load_d.wait()
    odd = (
        lax.broadcasted_iota(jnp.int32, (Y, Z), 0) + lax.broadcasted_iota(jnp.int32, (Y, Z), 1)
    ) % 2 == 1
    for j in range(X // 2):
        pm[3 + j, R : R + Y, 0:Z] = jnp.where(odd, own[2 * j], own[2 * j + 1])

    sems = iter(range(200))

    def pack(items, pk):
        base = 0
        sy = items[0][3][1]
        lane = lax.broadcasted_iota(jnp.int32, (sy, 128), 1)
        head = tail = jnp.zeros((sy, 128), jnp.float32)
        for buf, h, H, (sx, sy, sz), deep in items:
            for q in range(sx):
                v = buf[H + q, R : R + sy, 0:128]
                at = base + q * deep
                inside = (lane >= at) & (lane < at + deep)
                tail = jnp.where(inside, pltpu.roll(v, (at - (sz - deep)) % 128, 1), tail)
                head = jnp.where(inside, pltpu.roll(v, at, 1) if at else v, head)
            base += sx * deep
        assert base <= 128
        pk[0] = tail
        pk[1] = head

    def exchange(items, pk, rk):
        copies = []

        def send(src, dst, dx, dy, dz):
            k = next(sems)
            to = (lax.rem(ix + dx + nx, nx), lax.rem(iy + dy + ny, ny), lax.rem(iz + dz + nz, nz))
            copy = pltpu.make_async_remote_copy(
                src_ref=src, dst_ref=dst, send_sem=ssem.at[k], recv_sem=rsem.at[k],
                device_id=to, device_id_type=MESH,
            )
            copy.start()
            copies.append(copy)

        sy = items[0][3][1]
        rows_from = {0: pl.ds(R, sy), 1: pl.ds(sy, R), -1: pl.ds(R, R)}
        rows_to = {0: pl.ds(R, sy), 1: pl.ds(0, R), -1: pl.ds(R + sy, R)}
        for dx in (1, -1, 0):
            for dy in (1, -1, 0):
                for dz in (1, -1):
                    if dx == -1 and nx == 2:
                        continue
                    side = 0 if dz == 1 else 1
                    count = R if dy else sy
                    first = sy - R if dy == 1 else 0
                    send(
                        pk.at[side, pl.ds(first, count)],
                        rk.at[side, 1 - dx, 1 - dy, pl.ds(0, count)],
                        dx, dy, dz,
                    )
                if dx == 0 and dy == 0:
                    continue
                for buf, h, H, (sx, sy, sz), deep in items:
                    p_from = {0: pl.ds(H, sx), 1: pl.ds(H + sx - h, h), -1: pl.ds(H, h)}[dx]
                    p_to = {0: pl.ds(H, sx), 1: pl.ds(H - h, h), -1: pl.ds(H + sx, h)}[dx]
                    lanes = pl.ds(0, 128)
                    send(buf.at[p_from, rows_from[dy], lanes], buf.at[p_to, rows_to[dy], lanes], dx, dy, 0)
        return functools.partial(finish, items, rk, copies)

    def finish(items, rk, copies):
        for copy in copies:
            copy.wait()
        received = {}
        for group in range(3):
            slot = 0 if nx == 2 and group == 2 else group
            for side in range(2):
                received[side, group] = jnp.concatenate(
                    [rk[side, slot, 0, 0:R], rk[side, slot, 1], rk[side, slot, 2, 0:R]], axis=0
                )
        base = 0
        for buf, h, H, (sx, sy, sz), deep in items:
            rows = sy + 2 * R
            lane = lax.broadcasted_iota(jnp.int32, (rows, 128), 1)
            wide = sz == 128
            put = 0 if wide else sz
            for j in range(sx + 2 * h):
                group, q = (0, sx - h + j) if j < h else ((1, j - h) if j < h + sx else (2, j - h - sx))
                at = base + q * deep
                edge = jnp.where(
                    lane >= 112,
                    pltpu.roll(received[0, group], (128 - deep - at) % 128, 1),
                    pltpu.roll(received[1, group], (put - at) % 128, 1),
                )
                if wide:
                    buf[H - h + j, :, 128:256] = edge
                else:
                    buf[H - h + j] = jnp.where(lane < sz, buf[H - h + j], edge)
            base += sx * deep

    sixth = jnp.float32(1.0 / 6.0)

    def masks(rows, lanes):
        even = (
            lax.broadcasted_iota(jnp.int32, (rows, lanes), 0)
            + lax.broadcasted_iota(jnp.int32, (rows, lanes), 1)
        ) % 2 == 0
        return even, jnp.logical_not(even)

    def beside(a, p, c, index=lambda p: p):
        rows, lanes = c.shape
        t = a[index(p - 1)] + a[index(p + 1)]
        t = t + (pltpu.roll(c, 1, 0) + pltpu.roll(c, rows - 1, 0))
        return t + (pltpu.roll(c, 1, 1) + pltpu.roll(c, lanes - 1, 1))

    def half(a, b, s, lo, hi, H, off, colour, mask, shift=None, index=lambda p: p):
        for p in range(lo, hi):
            c = a[index(p)]
            t = beside(a, p, c, index) - s[p + off]
            if shift is not None:
                t = t + shift
            b[p] = jnp.where(mask[(p - H + colour) % 2], t * sixth, c)

    fine_mask = masks(Y + 2 * R, 2 * Z)
    one_mask = masks(y1 + 2 * R, 128)

    first = [(pm, 3, 3, (X // 2, Y, Z), 5), (den, 4, 6, (X, Y, Z), 4)]
    pack(first, pk_p)
    pl.semaphore_wait(barrier, n - 1)
    exchange(first, pk_p, rk_p)()
    for k, (a, b) in enumerate(((pm, pb), (pb, pa), (pa, pb), (pb, pa))):
        d = 4 - k
        index = (lambda p: p // 2) if k == 0 else (lambda p: p)
        half(a, b, den, 6 - d, 6 + X + d, 6, 0, k % 2, fine_mask, None, index)
    pairs = []
    total = jnp.zeros((Y, Z), jnp.float32)
    for q in range(x1):
        both = None
        for p in (6 + 2 * q, 7 + 2 * q):
            c = pa[p]
            left = (den[p] - (beside(pa, p, c) - 6.0 * c))[R : R + Y, 0:Z]
            both = left if both is None else both + left
            total = total + den[p, R : R + Y, 0:Z]
        f2[2 + q, R : R + Y, 0:Z] = jnp.where(
            odd, pa[6 + 2 * q, R : R + Y, 0:Z], pa[7 + 2 * q, R : R + Y, 0:Z]
        )
        pairs.append(both)
    stacked = jnp.concatenate(pairs, axis=0)
    stacked = jnp.dot(stacked, sz_ref[...], precision=HI, preferred_element_type=jnp.float32)
    one = jnp.dot(sy_ref[...], stacked, precision=HI, preferred_element_type=jnp.float32) * 0.5
    for q in range(x1):
        lv[6 + q, R : R + y1, :] = one[q * y1 : (q + 1) * y1]

    second = [(lv, 5, 6, (x1, y1, z1), 5)]
    pack(second, pk_l)
    exchange(second, pk_l, rk_l)()
    for p in range(6 - 4, 6 + x1 + 4):
        ea[p] = jnp.where(one_mask[p % 2], lv[p] * -sixth, 0.0)
    for k, (a, b) in enumerate(((ea, eb), (eb, ea), (ea, eb))):
        d = 3 - k
        half(a, b, lv, 6 - d, 6 + x1 + d, 6, 0, (k + 1) % 2, one_mask)
    acc = jnp.zeros((y1, 128), jnp.float32)
    for p in range(6, 6 + x1):
        c = eb[p]
        acc = acc + (lv[p] - (beside(eb, p, c) - 6.0 * c))[R : R + y1]
    for j in range(x1 // 2):
        e2[3 + j, R : R + y1, :] = jnp.where(
            odd[0:y1], eb[6 + 2 * j, R : R + y1], eb[7 + 2 * j, R : R + y1]
        )
    lane = lax.broadcasted_iota(jnp.int32, (y1, 128), 1)
    acc = jnp.where(lane < z1, acc, 0.0)

    def whole_sum(v):
        return jnp.sum(jnp.sum(v, axis=0, keepdims=True), axis=1, keepdims=True)

    gat[me, :, 0:128] = jnp.broadcast_to(whole_sum(acc), (1, 128))
    gat[me, :, 128:256] = jnp.broadcast_to(whole_sum(total), (1, 128))

    def spread(o, carry):
        pltpu.make_async_remote_copy(
            src_ref=gat.at[me], dst_ref=gat.at[me], send_sem=gs, recv_sem=gr,
            device_id=device(o), device_id_type=MESH,
        ).start()
        return carry

    lax.fori_loop(1, n, spread, 0)
    third = [(e2, 3, 3, (x1 // 2, y1, z1), 6)]
    fourth = [(f2, 2, 2, (X // 2, Y, Z), 4)]
    pack(third, pk_e)
    pack(fourth, pk_f)
    finish_third = exchange(third, pk_e, rk_e)
    finish_fourth = exchange(fourth, pk_f, rk_f)
    finish_third()
    finish_fourth()
    others = gat.at[pl.ds(0, n - 1)]
    pltpu.make_async_copy(others, others, gs).wait()
    pltpu.make_async_copy(others, others, gr).wait()

    values = gat[:, 0, :]
    blocks = values[:, 0:128]
    mean = jnp.sum(values[:, 128:256], axis=0, keepdims=True) / jnp.float32(n * X * Y * Z)
    blocks = blocks - jnp.sum(blocks, axis=0, keepdims=True) / jnp.float32(n)
    cv[...] = jnp.dot(op_ref[...], blocks, precision=HI, preferred_element_type=jnp.float32)
    row = lax.broadcasted_iota(jnp.int32, (y1 + 2 * R, 128), 0)
    lane = lax.broadcasted_iota(jnp.int32, (y1 + 2 * R, 128), 1)
    maps = []
    for dx in (-1, 0, 1):
        by_row = []
        for dy in (-1, 0, 1):
            vals = []
            for dz in (-1, 0, 1):
                at = (lax.rem(ix + dx + nx, nx) * ny + lax.rem(iy + dy + ny, ny)) * nz
                vals.append(cv[pl.ds(at + lax.rem(iz + dz + nz, nz), 1), :])
            by_row.append(jnp.where(lane < z1, vals[1], jnp.where(lane < (z1 + 128) // 2, vals[2], vals[0])))
        maps.append(jnp.where(row < R, by_row[0], jnp.where(row < R + y1, by_row[1], by_row[2])))
    for p in range(0, x1 + 12):
        which = 0 if p < 6 else (1 if p < 6 + x1 else 2)
        ea[p] = e2[p // 2] + (maps[which] + mean * jnp.float32(8.0 / 3.0))
    for k, (a, b) in enumerate(((ea, eb), (eb, ea), (ea, eb), (eb, ea))):
        d = 5 - k
        half(a, b, lv, 6 - d, 6 + x1 + d, 6, 0, k % 2, one_mask, 4.0 * mean)

    mean2 = jnp.concatenate([mean, mean], axis=1)
    for q in range(4, 6 + x1 + 2):
        wide = jnp.dot(ea[q], rz_ref[...], precision=HI, preferred_element_type=jnp.float32)
        wide = jnp.dot(ry_ref[...], wide, precision=HI, preferred_element_type=jnp.float32)
        wide = wide + mean2 * jnp.float32(2.0 / 3.0)
        for p in (2 * (q - 4), 2 * (q - 4) + 1):
            pb[p] = f2[p // 2] + wide
    for k, (a, b) in enumerate(((pb, pa), (pa, pb), (pb, pa))):
        d = 3 - k
        half(a, b, den, 4 - d, 4 + X + d, 4, 2, k % 2, fine_mask, mean2)
    for p in range(4, 4 + X):
        c = pa[p]
        t = (beside(pa, p, c) - den[p + 2] + mean2) * sixth
        out_ref[p - 4] = jnp.where(fine_mask[(p - 3) % 2], t, c)[R : R + Y, 0:Z]


def body(dims, density, potential):
    nx, ny, nz, X, Y, Z = dims
    n = nx * ny * nz
    x1, y1, z1 = X // 2, Y // 2, Z // 2
    op = coarse_operator(nx, ny, nz, float(y1 * z1), float(x1 * z1), float(x1 * y1))
    sz = (np.arange(Z)[:, None] // 2 == np.arange(128)[None, :]).astype(np.float32)
    r = np.arange(x1 * y1)
    c = np.arange(x1 * Y)
    sy = (r[:, None] == c[None, :] // 2).astype(np.float32)
    rz = (np.arange(128)[:, None] == np.arange(2 * Z)[None, :] // 2).astype(np.float32)
    rows, rows1 = Y + 2 * R, y1 + 2 * R
    ry = (np.arange(rows)[:, None] // 2 + R // 2 == np.arange(rows1)[None, :]).astype(np.float32)
    f32 = jnp.float32
    fine, one = (Y, 128), (y1, 128)
    vmem = pl.BlockSpec(memory_space=pltpu.VMEM)
    return pl.pallas_call(
        functools.partial(kernel, dims),
        out_shape=jax.ShapeDtypeStruct((X, Y, Z), f32),
        in_specs=[pl.BlockSpec(memory_space=pl.ANY)] * 2 + [vmem] * 5,
        out_specs=vmem,
        scratch_shapes=[
            pltpu.VMEM((X, Y, Z), f32),
            pltpu.VMEM((X // 2 + 6, rows, 2 * Z), f32),
            pltpu.VMEM((X + 12, rows, 2 * Z), f32),
            pltpu.VMEM((X + 12, rows, 2 * Z), f32),
            pltpu.VMEM((X + 12, rows, 2 * Z), f32),
            pltpu.VMEM((x1 + 12, rows1, 128), f32),
            pltpu.VMEM((x1 + 12, rows1, 128), f32),
            pltpu.VMEM((x1 + 12, rows1, 128), f32),
            pltpu.VMEM((x1 // 2 + 6, rows1, 128), f32),
            pltpu.VMEM((X // 2 + 4, rows, 2 * Z), f32),
            pltpu.VMEM((n, 1, 256), f32),
            pltpu.VMEM((n, 128), f32),
        ]
        + [pltpu.VMEM(lead + s, f32) for lead in ((2,), (2, 3, 3)) for s in (fine, one, one, fine)]
        + [
            pltpu.SemaphoreType.DMA((120,)),
            pltpu.SemaphoreType.DMA((120,)),
            pltpu.SemaphoreType.DMA,
            pltpu.SemaphoreType.DMA,
            pltpu.SemaphoreType.DMA((2,)),
        ],
        compiler_params=pltpu.CompilerParams(collective_id=0, has_side_effects=True),
        name="vcycle",
    )(density, potential, op, sz, sy, rz, ry)


def solution(mesh):
    nx, ny, nz = (mesh.shape[a] for a in ("gx", "gy", "gz"))

    def run(density, potential):
        return body((nx, ny, nz) + density.shape, density, potential)

    spec = P("gx", "gy", "gz")
    return jax.shard_map(run, mesh=mesh, in_specs=(spec, spec), out_specs=spec, check_vma=False)
```

time: 59.7 us -> 40.9 us (0.69)
  Pallas kernels: 57.8 us -> 39.2 us
    pallas_call x1, Pallas kernels: 57.8 us -> 39.2 us  [body(): pl.pallas_call(functools.partial(kernel, dims), out_shape=jax.ShapeDtypeS...]
where the time goes in v2:
time: 40.9 us; the launch traced here: 40.7 us
  Pallas kernels  39.2 us (96%)
  local copies, waits for them, and re-layouts  1.54 us (4%)
    pallas_call x1, Pallas kernels, body(): pl.pallas_call(functools.partial(kernel, dims), out_shape=jax.ShapeDtypeS...  39.2 us
    unnamed x1, local copies, waits for them, and re-layouts  1.54 us

profile of v2, /device:TPU:0, one launch (start us, length us, event | category | flops | bytes accessed | tf_op | source)
XLA Modules:
  0.0 40.7 jit_solution(8293206501630962259)
XLA Ops:
  0.0 39.2 %vcycle.1 = f32[12,16,128]{2,1,0:T(8,128)} custom-call(f32[12,16,128]{2,1,0:T(8,128)} %den_hbm.1, f32[12,16,128]{2,1,0:T(8,128)} %pot_hbm.1, f32[32,32]{1,0:T(8,128)} %constant.10.clone.op_ref, f32[128,128]{1,0:T(8,128)} %constant.11.clone.sz_ref, f32[48,96]{1,0:T(8,128)} %constant.12.clone.sy_ref, f32[128,256]{1,0:T(8,128)} %constant.13.clone.rz_ref, ...), custom_call_target="tpu_custom_call" | custom-call | tf_op jit(solution)/shard_map/vcycle/pallas_call | solution.py:312
  39.2 1.5 %copy.9 = f32[12,16,128]{2,1,0:T(8,128)} copy(f32[12,16,128]{2,1,0:T(8,128)} %vcycle.1) | data formatting | bytes 196608

commit v3 on v2

--- a/solution.py
+++ b/solution.py
@@ -34,7 +34,7 @@
 
 
 def kernel(
-    dims, den_hbm, pot_hbm, op_ref, sz_ref, sy_ref, rz_ref, ry_ref, out_ref,
+    dims, den_hbm, pot_hbm, op_hbm, out_ref, op_ref,
     own, pm, pa, pb, den, lv, ea, eb, e2, f2, gat, cv,
     pk_p, pk_l, pk_e, pk_f, rk_p, rk_l, rk_e, rk_f,
     ssem, rsem, gs, gr, lsem,
@@ -45,14 +45,30 @@
     ix, iy, iz = lax.axis_index("gx"), lax.axis_index("gy"), lax.axis_index("gz")
     me = (ix * ny + iy) * nz + iz
 
+    def around(i, count):
+        return [i] + [jnp.where(i + o >= count, i + o - count, i + o) for o in range(1, count)]
+
+    xs, ys, zs = around(ix, nx), around(iy, ny), around(iz, nz)
+
     def device(o):
+        if isinstance(o, int):
+            return (xs[o // (ny * nz)], ys[o // nz % ny], zs[o % nz])
         ox, oy, oz = o // (ny * nz), (o // nz) % ny, o % nz
         return (lax.rem(ix + ox, nx), lax.rem(iy + oy, ny), lax.rem(iz + oz, nz))
+
+    def each_other(step):
+        if n <= 64:
+            for o in range(1, n):
+                step(o, 0)
+        else:
+            lax.fori_loop(1, n, step, 0)
 
     load_p = pltpu.make_async_copy(pot_hbm, own, lsem.at[0])
     load_d = pltpu.make_async_copy(den_hbm, den.at[pl.ds(6, X), pl.ds(R, Y), pl.ds(0, Z)], lsem.at[1])
     load_p.start()
     load_d.start()
+    load_op = pltpu.make_async_copy(op_hbm, op_ref, lsem.at[2])
+    load_op.start()
 
     barrier = pltpu.get_barrier_semaphore()
 
@@ -60,7 +76,7 @@
         pl.semaphore_signal(barrier, inc=1, device_id=device(o), device_id_type=MESH)
         return carry
 
-    lax.fori_loop(1, n, greet, 0)
+    each_other(greet)
     load_p.wait()
     load_d.wait()
     odd = (
@@ -93,7 +109,7 @@
 
         def send(src, dst, dx, dy, dz):
             k = next(sems)
-            to = (lax.rem(ix + dx + nx, nx), lax.rem(iy + dy + ny, ny), lax.rem(iz + dz + nz, nz))
+            to = (xs[dx], ys[dy], zs[dz])
             copy = pltpu.make_async_remote_copy(
                 src_ref=src, dst_ref=dst, send_sem=ssem.at[k], recv_sem=rsem.at[k],
                 device_id=to, device_id_type=MESH,
@@ -203,9 +219,15 @@
             odd, pa[6 + 2 * q, R : R + Y, 0:Z], pa[7 + 2 * q, R : R + Y, 0:Z]
         )
         pairs.append(both)
+    def halves(shape, dim, start=0):
+        i = [lax.broadcasted_iota(jnp.int32, shape, k) for k in (0, 1)]
+        return jnp.where((i[dim] >> 1) + start == i[1 - dim], 1.0, 0.0).astype(jnp.float32)
+
+    to_z, to_y = halves((Z, 128), 0), halves((x1 * y1, x1 * Y), 1)
+    from_z, from_y = halves((128, 2 * Z), 1), halves((Y + 2 * R, y1 + 2 * R), 0, R // 2)
     stacked = jnp.concatenate(pairs, axis=0)
-    stacked = jnp.dot(stacked, sz_ref[...], precision=HI, preferred_element_type=jnp.float32)
-    one = jnp.dot(sy_ref[...], stacked, precision=HI, preferred_element_type=jnp.float32) * 0.5
+    stacked = jnp.dot(stacked, to_z, precision=HI, preferred_element_type=jnp.float32)
+    one = jnp.dot(to_y, stacked, precision=HI, preferred_element_type=jnp.float32) * 0.5
     for q in range(x1):
         lv[6 + q, R : R + y1, :] = one[q * y1 : (q + 1) * y1]
 
@@ -241,7 +263,7 @@
         ).start()
         return carry
 
-    lax.fori_loop(1, n, spread, 0)
+    each_other(spread)
     third = [(e2, 3, 3, (x1 // 2, y1, z1), 6)]
     fourth = [(f2, 2, 2, (X // 2, Y, Z), 4)]
     pack(third, pk_e)
@@ -254,6 +276,7 @@
     pltpu.make_async_copy(others, others, gs).wait()
     pltpu.make_async_copy(others, others, gr).wait()
 
+    load_op.wait()
     values = gat[:, 0, :]
     blocks = values[:, 0:128]
     mean = jnp.sum(values[:, 128:256], axis=0, keepdims=True) / jnp.float32(n * X * Y * Z)
@@ -267,8 +290,8 @@
         for dy in (-1, 0, 1):
             vals = []
             for dz in (-1, 0, 1):
-                at = (lax.rem(ix + dx + nx, nx) * ny + lax.rem(iy + dy + ny, ny)) * nz
-                vals.append(cv[pl.ds(at + lax.rem(iz + dz + nz, nz), 1), :])
+                at = (xs[dx] * ny + ys[dy]) * nz
+                vals.append(cv[pl.ds(at + zs[dz], 1), :])
             by_row.append(jnp.where(lane < z1, vals[1], jnp.where(lane < (z1 + 128) // 2, vals[2], vals[0])))
         maps.append(jnp.where(row < R, by_row[0], jnp.where(row < R + y1, by_row[1], by_row[2])))
     for p in range(0, x1 + 12):
@@ -280,8 +303,8 @@
 
     mean2 = jnp.concatenate([mean, mean], axis=1)
     for q in range(4, 6 + x1 + 2):
-        wide = jnp.dot(ea[q], rz_ref[...], precision=HI, preferred_element_type=jnp.float32)
-        wide = jnp.dot(ry_ref[...], wide, precision=HI, preferred_element_type=jnp.float32)
+        wide = jnp.dot(ea[q], from_z, precision=HI, preferred_element_type=jnp.float32)
+        wide = jnp.dot(from_y, wide, precision=HI, preferred_element_type=jnp.float32)
         wide = wide + mean2 * jnp.float32(2.0 / 3.0)
         for p in (2 * (q - 4), 2 * (q - 4) + 1):
             pb[p] = f2[p // 2] + wide
@@ -299,22 +322,17 @@
     n = nx * ny * nz
     x1, y1, z1 = X // 2, Y // 2, Z // 2
     op = coarse_operator(nx, ny, nz, float(y1 * z1), float(x1 * z1), float(x1 * y1))
-    sz = (np.arange(Z)[:, None] // 2 == np.arange(128)[None, :]).astype(np.float32)
-    r = np.arange(x1 * y1)
-    c = np.arange(x1 * Y)
-    sy = (r[:, None] == c[None, :] // 2).astype(np.float32)
-    rz = (np.arange(128)[:, None] == np.arange(2 * Z)[None, :] // 2).astype(np.float32)
     rows, rows1 = Y + 2 * R, y1 + 2 * R
-    ry = (np.arange(rows)[:, None] // 2 + R // 2 == np.arange(rows1)[None, :]).astype(np.float32)
     f32 = jnp.float32
     fine, one = (Y, 128), (y1, 128)
     vmem = pl.BlockSpec(memory_space=pltpu.VMEM)
     return pl.pallas_call(
         functools.partial(kernel, dims),
         out_shape=jax.ShapeDtypeStruct((X, Y, Z), f32),
-        in_specs=[pl.BlockSpec(memory_space=pl.ANY)] * 2 + [vmem] * 5,
+        in_specs=[pl.BlockSpec(memory_space=pl.ANY)] * 3,
         out_specs=vmem,
         scratch_shapes=[
+            pltpu.VMEM((n, n), f32),
             pltpu.VMEM((X, Y, Z), f32),
             pltpu.VMEM((X // 2 + 6, rows, 2 * Z), f32),
             pltpu.VMEM((X + 12, rows, 2 * Z), f32),
@@ -334,11 +352,11 @@
             pltpu.SemaphoreType.DMA((120,)),
             pltpu.SemaphoreType.DMA,
             pltpu.SemaphoreType.DMA,
-            pltpu.SemaphoreType.DMA((2,)),
+            pltpu.SemaphoreType.DMA((3,)),
         ],
         compiler_params=pltpu.CompilerParams(collective_id=0, has_side_effects=True),
         name="vcycle",
-    )(density, potential, op, sz, sy, rz, ry)
+    )(density, potential, op)
 
 
 def solution(mesh):

time: 40.9 us -> 39.2 us (0.958)
  Pallas kernels: 39.2 us -> 37.5 us
    pallas_call x1, Pallas kernels: 39.2 us -> 37.5 us  [body(): pl.pallas_call(functools.partial(kernel, dims), out_shape=jax.ShapeDtypeS...]
where the time goes in v3:
time: 39.2 us; the launch traced here: 39 us
  Pallas kernels  37.5 us (96%)
  local copies, waits for them, and re-layouts  1.54 us (4%)
    pallas_call x1, Pallas kernels, body(): pl.pallas_call(functools.partial(kernel, dims), out_shape=jax.ShapeDtypeS...  37.5 us
    unnamed x1, local copies, waits for them, and re-layouts  1.54 us

profile of v3, /device:TPU:0, one launch (start us, length us, event | category | flops | bytes accessed | tf_op | source)
XLA Modules:
  0.0 39.0 jit_solution(8102517024178391885)
XLA Ops:
  0.0 37.5 %vcycle.1 = f32[12,16,128]{2,1,0:T(8,128)} custom-call(f32[12,16,128]{2,1,0:T(8,128)} %den_hbm.1, f32[12,16,128]{2,1,0:T(8,128)} %pot_hbm.1, f32[32,32]{1,0:T(8,128)} %constant.2.clone.op_hbm), custom_call_target="tpu_custom_call" | custom-call | tf_op jit(solution)/shard_map/vcycle/pallas_call | solution.py:329
  37.5 1.5 %copy.5 = f32[12,16,128]{2,1,0:T(8,128)} copy(f32[12,16,128]{2,1,0:T(8,128)} %vcycle.1) | data formatting | bytes 196608

commit v4 on v3

--- a/solution.py
+++ b/solution.py
@@ -76,7 +76,16 @@
         pl.semaphore_signal(barrier, inc=1, device_id=device(o), device_id_type=MESH)
         return carry
 
-    each_other(greet)
+    near = max(nx, ny, nz) <= 5
+    steps = sorted({
+        (dx % nx * ny + dy % ny) * nz + dz % nz
+        for dx in (-1, 0, 1) for dy in (-1, 0, 1) for dz in (-1, 0, 1)
+    } - {0})
+    if near:
+        for o in steps:
+            greet(o, 0)
+    else:
+        each_other(greet)
     load_p.wait()
     load_d.wait()
     odd = (
@@ -200,7 +209,7 @@
 
     first = [(pm, 3, 3, (X // 2, Y, Z), 5), (den, 4, 6, (X, Y, Z), 4)]
     pack(first, pk_p)
-    pl.semaphore_wait(barrier, n - 1)
+    pl.semaphore_wait(barrier, len(steps) if near else n - 1)
     exchange(first, pk_p, rk_p)()
     for k, (a, b) in enumerate(((pm, pb), (pb, pa), (pa, pb), (pb, pa))):
         d = 4 - k
@@ -233,7 +242,11 @@
 
     second = [(lv, 5, 6, (x1, y1, z1), 5)]
     pack(second, pk_l)
-    exchange(second, pk_l, rk_l)()
+    finish_second = exchange(second, pk_l, rk_l)
+    fourth = [(f2, 2, 2, (X // 2, Y, Z), 4)]
+    pack(fourth, pk_f)
+    finish_fourth = exchange(fourth, pk_f, rk_f)
+    finish_second()
     for p in range(6 - 4, 6 + x1 + 4):
         ea[p] = jnp.where(one_mask[p % 2], lv[p] * -sixth, 0.0)
     for k, (a, b) in enumerate(((ea, eb), (eb, ea), (ea, eb))):
@@ -265,11 +278,8 @@
 
     each_other(spread)
     third = [(e2, 3, 3, (x1 // 2, y1, z1), 6)]
-    fourth = [(f2, 2, 2, (X // 2, Y, Z), 4)]
     pack(third, pk_e)
-    pack(fourth, pk_f)
     finish_third = exchange(third, pk_e, rk_e)
-    finish_fourth = exchange(fourth, pk_f, rk_f)
     finish_third()
     finish_fourth()
     others = gat.at[pl.ds(0, n - 1)]

time: 39.2 us -> 38 us (0.969)
  Pallas kernels: 37.5 us -> 36.3 us
    pallas_call x1, Pallas kernels: 37.5 us -> 36.3 us  [body(): pl.pallas_call(functools.partial(kernel, dims), out_shape=jax.ShapeDtypeS...]
where the time goes in v4:
time: 38 us; the launch traced here: 37.8 us
  Pallas kernels  36.3 us (96%)
  local copies, waits for them, and re-layouts  1.54 us (4%)
    pallas_call x1, Pallas kernels, body(): pl.pallas_call(functools.partial(kernel, dims), out_shape=jax.ShapeDtypeS...  36.3 us
    unnamed x1, local copies, waits for them, and re-layouts  1.54 us

profile of v4, /device:TPU:0, one launch (start us, length us, event | category | flops | bytes accessed | tf_op | source)
XLA Modules:
  0.0 37.8 jit_solution(4616833940578563128)
XLA Ops:
  0.0 36.3 %vcycle.1 = f32[12,16,128]{2,1,0:T(8,128)} custom-call(f32[12,16,128]{2,1,0:T(8,128)} %den_hbm.1, f32[12,16,128]{2,1,0:T(8,128)} %pot_hbm.1, f32[32,32]{1,0:T(8,128)} %constant.2.clone.op_hbm), custom_call_target="tpu_custom_call" | custom-call | tf_op jit(solution)/shard_map/vcycle/pallas_call | solution.py:339
  36.3 1.5 %copy.5 = f32[12,16,128]{2,1,0:T(8,128)} copy(f32[12,16,128]{2,1,0:T(8,128)} %vcycle.1) | data formatting | bytes 196608

commit v5 on v4

--- a/solution.py
+++ b/solution.py
@@ -112,6 +112,9 @@
         assert base <= 128
         pk[0] = tail
         pk[1] = head
+
+    def once(h, H, sx):
+        return nx == 2 and 2 * h > sx and H >= sx
 
     def exchange(items, pk, rk):
         copies = []
@@ -145,6 +148,10 @@
                 if dx == 0 and dy == 0:
                     continue
                 for buf, h, H, (sx, sy, sz), deep in items:
+                    if once(h, H, sx):
+                        if dx == -1:
+                            continue
+                        h = sx if dx else h
                     p_from = {0: pl.ds(H, sx), 1: pl.ds(H + sx - h, h), -1: pl.ds(H, h)}[dx]
                     p_to = {0: pl.ds(H, sx), 1: pl.ds(H - h, h), -1: pl.ds(H + sx, h)}[dx]
                     lanes = pl.ds(0, 128)
@@ -166,6 +173,7 @@
             rows = sy + 2 * R
             lane = lax.broadcasted_iota(jnp.int32, (rows, 128), 1)
             wide = sz == 128
+            assert not (wide and once(h, H, sx))
             put = 0 if wide else sz
             for j in range(sx + 2 * h):
                 group, q = (0, sx - h + j) if j < h else ((1, j - h) if j < h + sx else (2, j - h - sx))
@@ -178,7 +186,8 @@
                 if wide:
                     buf[H - h + j, :, 128:256] = edge
                 else:
-                    buf[H - h + j] = jnp.where(lane < sz, buf[H - h + j], edge)
+                    at = H - sx + q if group == 2 and once(h, H, sx) else H - h + j
+                    buf[H - h + j] = jnp.where(lane < sz, buf[at], edge)
             base += sx * deep
 
     sixth = jnp.float32(1.0 / 6.0)

time: 38 us -> 36.8 us (0.968)
  Pallas kernels: 36.3 us -> 35.1 us
    pallas_call x1, Pallas kernels: 36.3 us -> 35.1 us  [body(): pl.pallas_call(functools.partial(kernel, dims), out_shape=jax.ShapeDtypeS...]
where the time goes in v5:
time: 36.8 us; the launch traced here: 36.6 us
  Pallas kernels  35.1 us (95%)
  local copies, waits for them, and re-layouts  1.54 us (4%)
    pallas_call x1, Pallas kernels, body(): pl.pallas_call(functools.partial(kernel, dims), out_shape=jax.ShapeDtypeS...  35.1 us
    unnamed x1, local copies, waits for them, and re-layouts  1.54 us

profile of v5, /device:TPU:0, one launch (start us, length us, event | category | flops | bytes accessed | tf_op | source)
XLA Modules:
  0.0 36.6 jit_solution(13083316198882938819)
XLA Ops:
  0.0 35.1 %vcycle.1 = f32[12,16,128]{2,1,0:T(8,128)} custom-call(f32[12,16,128]{2,1,0:T(8,128)} %den_hbm.1, f32[12,16,128]{2,1,0:T(8,128)} %pot_hbm.1, f32[32,32]{1,0:T(8,128)} %constant.2.clone.op_hbm), custom_call_target="tpu_custom_call" | custom-call | tf_op jit(solution)/shard_map/vcycle/pallas_call | solution.py:348
  35.1 1.5 %copy.5 = f32[12,16,128]{2,1,0:T(8,128)} copy(f32[12,16,128]{2,1,0:T(8,128)} %vcycle.1) | data formatting | bytes 196608

commit v6 on v5

--- a/solution.py
+++ b/solution.py
@@ -255,6 +255,10 @@
     fourth = [(f2, 2, 2, (X // 2, Y, Z), 4)]
     pack(fourth, pk_f)
     finish_fourth = exchange(fourth, pk_f, rk_f)
+    def whole_sum(v):
+        return jnp.sum(jnp.sum(v, axis=0, keepdims=True), axis=1, keepdims=True)
+
+    gat[me, :, 128:256] = jnp.broadcast_to(whole_sum(total), (1, 128))
     finish_second()
     for p in range(6 - 4, 6 + x1 + 4):
         ea[p] = jnp.where(one_mask[p % 2], lv[p] * -sixth, 0.0)
@@ -272,11 +276,7 @@
     lane = lax.broadcasted_iota(jnp.int32, (y1, 128), 1)
     acc = jnp.where(lane < z1, acc, 0.0)
 
-    def whole_sum(v):
-        return jnp.sum(jnp.sum(v, axis=0, keepdims=True), axis=1, keepdims=True)
-
     gat[me, :, 0:128] = jnp.broadcast_to(whole_sum(acc), (1, 128))
-    gat[me, :, 128:256] = jnp.broadcast_to(whole_sum(total), (1, 128))
 
     def spread(o, carry):
         pltpu.make_async_remote_copy(
@@ -289,8 +289,8 @@
     third = [(e2, 3, 3, (x1 // 2, y1, z1), 6)]
     pack(third, pk_e)
     finish_third = exchange(third, pk_e, rk_e)
+    finish_fourth()
     finish_third()
-    finish_fourth()
     others = gat.at[pl.ds(0, n - 1)]
     pltpu.make_async_copy(others, others, gs).wait()
     pltpu.make_async_copy(others, others, gr).wait()

time: 36.8 us -> 36.6 us (level)
  no operation moved by 1% of the time
where the time goes in v6:
time: 36.6 us; the launch traced here: 36.4 us
  Pallas kernels  34.9 us (95%)
  local copies, waits for them, and re-layouts  1.54 us (4%)
    pallas_call x1, Pallas kernels, body(): pl.pallas_call(functools.partial(kernel, dims), out_shape=jax.ShapeDtypeS...  34.9 us
    unnamed x1, local copies, waits for them, and re-layouts  1.54 us

profile of v6, /device:TPU:0, one launch (start us, length us, event | category | flops | bytes accessed | tf_op | source)
XLA Modules:
  0.0 36.4 jit_solution(16150756542611232096)
XLA Ops:
  0.0 34.9 %vcycle.1 = f32[12,16,128]{2,1,0:T(8,128)} custom-call(f32[12,16,128]{2,1,0:T(8,128)} %den_hbm.1, f32[12,16,128]{2,1,0:T(8,128)} %pot_hbm.1, f32[32,32]{1,0:T(8,128)} %constant.2.clone.op_hbm), custom_call_target="tpu_custom_call" | custom-call | tf_op jit(solution)/shard_map/vcycle/pallas_call | solution.py:348
  34.9 1.5 %copy.5 = f32[12,16,128]{2,1,0:T(8,128)} copy(f32[12,16,128]{2,1,0:T(8,128)} %vcycle.1) | data formatting | bytes 196608
